TPU v7x, 32 devices: a whole 2x2x4 slice. The times are simulated.
32 devices in a mesh: rep: 8 (over z, x), tp: 4 (over y, core).
Axes of the slice: x: 2, y: 2, z: 4, core: 2. Of those that a mesh axis runs over, the one named last changes fastest.
Arguments:
- stream_in: bfloat16 [32, 4, 8192], P('rep', None, 'tp'), may hold values from -6 to 6
- queries: bfloat16 [32, 4, 4096], P('rep'), may hold values from -90 to 90
- new_keys: bfloat16 [32, 4, 4, 128], P('rep'), may hold values from -4 to 4
- new_values: bfloat16 [32, 4, 4, 128], P('rep'), may hold values from -4 to 4
- key_cache: bfloat16 [32, 1024, 4, 128], P('rep', 'tp'), may hold values from -4.1 to 4.1
- value_cache: bfloat16 [32, 1024, 4, 128], P('rep', 'tp'), may hold values from -4 to 4
- lengths: int32 [32], P('rep'), may hold values from 2 to 1024
- out_weight: bfloat16 [4096, 8192], P('tp', 'rep'), may hold values from -0.09375 to 0.09375
- norm_gain: bfloat16 [8192], P('tp'), may hold values from 0.5 to 1.5
Outputs:
- stream_out: bfloat16 [32, 4, 8192], P('rep', None, 'tp')
- normed: bfloat16 [32, 4, 8192], P('rep', None, 'tp')
All inputs are finite; a program needn't handle non-finite values.
Results may differ from a plain program's by a relative error of at most 0.0065.
Values may be sent and summed in bfloat16 or wider, within the bound.
A program may use at most 64 MiB of HBM per device.

v0:
```python
import math

import jax
import jax.numpy as jnp
from jax import lax
from jax.sharding import PartitionSpec as P

D = 8192


def on_device(
    stream_in, queries, new_keys, new_values, key_cache, value_cache, lengths, out_weight, norm_gain
):
    row_count, step_count, width = queries.shape
    kv_heads, head_dim = (key_cache.shape[2], key_cache.shape[3])
    block_len = key_cache.shape[1]
    group_size = width // head_dim // kv_heads
    tp_index = lax.axis_index("tp")
    scaling = 1.0 / math.sqrt(head_dim)
    grouped = queries.reshape(row_count, step_count, kv_heads, group_size, head_dim)
    cached = (
        jnp.einsum("bsgjd,bpgd->bsgjp", grouped, key_cache, preferred_element_type=jnp.float32)
        * scaling
    )
    positions = tp_index * block_len + jnp.arange(block_len, dtype=jnp.int32)
    visible = positions[None, :] < lengths[:, None]
    cached = jnp.where(visible[:, None, None, None, :], cached, -1e30)
    fresh = (
        jnp.einsum("bsgjd,btgd->bsgjt", grouped, new_keys, preferred_element_type=jnp.float32)
        * scaling
    )
    causal = (jnp.arange(step_count)[None, :] <= jnp.arange(step_count)[:, None]) & (tp_index == 0)
    fresh = jnp.where(causal[None, :, None, None, :], fresh, -1e30)
    local_maxima = jnp.maximum(cached.max(-1), fresh.max(-1))
    maxima = lax.pmax(local_maxima, "tp")
    weights_cached = jnp.exp(cached - maxima[..., None])
    weights_fresh = jnp.exp(fresh - maxima[..., None])
    denominator = weights_cached.sum(-1) + weights_fresh.sum(-1)
    numerator = jnp.einsum(
        "bsgjp,bpgd->bsgjd",
        weights_cached.astype(jnp.bfloat16),
        value_cache,
        preferred_element_type=jnp.float32,
    )
    numerator = numerator + jnp.einsum(
        "bsgjt,btgd->bsgjd",
        weights_fresh.astype(jnp.bfloat16),
        new_values,
        preferred_element_type=jnp.float32,
    )
    numerator = numerator.reshape(row_count, step_count, kv_heads * group_size, head_dim)
    denominator = denominator.reshape(row_count, step_count, kv_heads * group_size)
    numerator, denominator = (
        lax.psum_scatter(
            numerator.astype(jnp.bfloat16), "tp", scatter_dimension=2, tiled=True
        ).astype(jnp.float32),
        lax.psum_scatter(
            denominator.astype(jnp.bfloat16), "tp", scatter_dimension=2, tiled=True
        ).astype(jnp.float32),
    )
    attended = (numerator / denominator[..., None]).astype(jnp.bfloat16)
    attended = attended.reshape(row_count * step_count, -1)
    projected = jnp.dot(
        lax.all_gather(attended, "rep", axis=0, tiled=True),
        out_weight,
        preferred_element_type=jnp.float32,
    ).astype(jnp.bfloat16)
    partial_value = lax.all_to_all(
        projected, "rep", split_axis=0, concat_axis=1, tiled=True
    ).astype(jnp.float32)
    summed = lax.psum_scatter(
        partial_value.astype(jnp.bfloat16), "tp", scatter_dimension=1, tiled=True
    ).astype(jnp.float32)
    hidden = stream_in.reshape(row_count * step_count, -1).astype(jnp.float32) + summed
    squares = lax.psum(jnp.sum(hidden * hidden, axis=1), "tp")
    inverse = lax.rsqrt(squares / D + 1e-06)
    normed = hidden * inverse[:, None] * norm_gain.astype(jnp.float32)[None, :]
    stream_out = hidden.astype(jnp.bfloat16).reshape(row_count, step_count, -1)
    return (stream_out, normed.astype(jnp.bfloat16).reshape(row_count, step_count, -1))


def solution(mesh):
    return jax.shard_map(
        on_device,
        mesh=mesh,
        in_specs=(
            P("rep", None, "tp"),
            P("rep", None, None),
            P("rep", None, None, None),
            P("rep", None, None, None),
            P("rep", "tp", None, None),
            P("rep", "tp", None, None),
            P("rep"),
            P("tp", "rep"),
            P("tp"),
        ),
        out_specs=(P("rep", None, "tp"), P("rep", None, "tp")),
        check_vma=False,
    )
```

profile of v0, /device:TPU:0, one launch (start us, length us, event | category | flops | bytes accessed | tf_op | source)
XLA Modules:
  0.0 127.4 jit_solution(1407445413883382145)
XLA Ops:
  7.2 0.0 copy-start
  7.2 0.0 copy-start.4
  7.2 0.0 reduce-scatter.8.cloned.1.call-start
  7.2 1.2 reshape.73
  8.5 0.7 broadcast_compare_fusion
  9.2 0.0 copy-start.2
  9.2 1.8 %fusion.23 = (f32[4,4,4,8]{3,1,2,0:T(4,128)S(1)}, f32[4,4,4,8,256]{4,3,1,2,0:T(8,128)S(1)}) fusion(bf16[4,4,4,8,128]{4,3,2,1,0:T(8,128)(2,1)S(1)} %reshape.73, bf16[4,256,4,128,1]{3,2,1,0,4:T(4,128)(2,1)} %bitcast.43, pred[4,256]{1,0:T(4,128)(4,1)S(1)} %broadcast_compare_fusion), kind=kOutput, calls=%fused_computation.40 | convolution fusion | flops 33947136 | bytes 1707008 | tf_op jit(solution)/shard_map/bsgjd,bpgd->bsgjp/dot_general | solution.py:22
  11.0 0.0 copy-done.4
  11.0 0.7 fusion.24
  11.7 12.9 %pmax.7 = f32[4,4,4,8]{3,1,2,0:T(4,128)S(1)} all-reduce(f32[4,4,4,8]{3,1,2,0:T(4,128)S(1)} %max.5), channel_id=1, replica_groups=mesh['rep'=8,'tp'=4] {'tp'}, use_global_device_ids=true, to_apply=%region_2.3 | all-reduce | flops 512 | bytes 4096 | tf_op jit(solution)/shard_map/pmax | solution.py:35
  24.7 0.0 copy-start.5
  24.7 1.5 %fusion.6 = f32[4,4,4,8,128]{4,3,2,1,0:T(8,128)S(1)} fusion(bf16[4,256,4,128,1]{3,2,1,0,4:T(4,128)(2,1)} %bitcast.33, f32[4,4,4,8,256]{4,3,1,2,0:T(8,128)S(1)} %get-tuple-element.5, f32[4,4,4,8]{3,1,2,0:T(4,128)S(1)} %pmax.7), kind=kOutput, calls=%fused_computation.10 | convolution fusion | flops 33816576 | bytes 1837056 | tf_op jit(solution)/shard_map/bsgjp,bpgd->bsgjd/dot_general | solution.py:39
  26.2 0.0 copy-done.2
  26.2 0.3 fusion.3
  26.5 0.1 copy.84
  26.6 0.7 reshape.82
  27.3 0.0 reduce-scatter.8.cloned.1.call-update
  27.3 0.0 reduce-scatter.6.cloned.1.call-start
  27.4 0.3 fusion.9
  27.7 0.1 fusion.15
  27.9 0.1 convert_element_type.62
  27.9 0.0 copy-done.5
  27.9 0.6 dynamic-slice
  29.2 5.8 %all-reduce = bf16[4,4,32]{2,1,0:T(4,128)(2,1)S(1)} all-reduce(bf16[4,4,32]{2,1,0:T(4,128)(2,1)S(1)} %convert_element_type.62), channel_id=3, replica_groups=mesh['rep'=8,'tp'=4] {'tp'}, use_global_device_ids=true, to_apply=%region_6.7.clone | all-reduce | flops 512 | bytes 2048
  35.0 0.1 dynamic-slice_convert_fusion
  35.0 12.4 %reduce-scatter.8.cloned.1.call-done = bf16[8,2048]{1,0:T(8,128)(2,1)} async-done(((bf16[32,2048]{1,0:T(8,128)(2,1)}), bf16[8,2048]{1,0:T(8,128)(2,1)}) %reduce-scatter.8.cloned.1.call-update) | async-done | bytes 32784
  47.4 0.8 reshape.83
  48.2 0.1 divide_convert_fusion
  48.3 0.0 copy-start.1
  48.3 30.9 %all_gather.3 = bf16[128,1024]{1,0:T(8,128)(2,1)S(1)} all-gather(bf16[16,1024]{1,0:T(8,128)(2,1)S(1)} %bitcast.39), channel_id=1, replica_groups=mesh['rep'=8,'tp'=4] {'rep'}, dimensions={0}, use_global_device_ids=true | all-gather | bytes 294912 | tf_op jit(solution)/shard_map/all_gather | solution.py:64
  79.2 0.0 copy-done
  79.2 0.0 copy-start.3
  79.2 0.4 convolution_convert_fusion
  79.7 13.5 %all_to_all.19 = bf16[8,16,1024]{2,1,0:T(8,128)(2,1)S(1)} all-to-all(bf16[8,16,1024]{2,1,0:T(8,128)(2,1)S(1)} %bitcast.34), channel_id=1, replica_groups=mesh['rep'=8,'tp'=4] {'rep'}, dimensions={0} | all-to-all | bytes 524288 | tf_op jit(solution)/shard_map/all_to_all | solution.py:68
  93.2 0.7 copy.58
  93.9 0.0 reduce-scatter.6.cloned.1.call-update
  93.9 0.0 copy-done.1
  94.0 0.0 copy-done.3
  94.0 17.5 %reduce-scatter.6.cloned.1.call-done = bf16[16,2048]{1,0:T(8,128)(2,1)} async-done(((bf16[16,8192]{1,0:T(8,128)(2,1)}), bf16[16,2048]{1,0:T(8,128)(2,1)}) %reduce-scatter.6.cloned.1.call-update) | async-done | bytes 65552 | tf_op jit(solution)/shard_map/reduce_scatter | solution.py:71
  111.5 1.0 multiply_reduce_fusion
  112.5 5.8 %psum.7 = f32[16]{0:T(128)S(1)} all-reduce(f32[16]{0:T(128)S(1)} %multiply_reduce_fusion), channel_id=1, replica_groups=mesh['rep'=8,'tp'=4] {'tp'}, use_global_device_ids=true, to_apply=%region_9.10 | all-reduce | flops 16 | bytes 128 | tf_op jit(solution)/shard_map/psum | solution.py:75
  118.3 0.9 multiply_convert_fusion
  119.2 0.7 reshape.75
  119.9 0.7 reshape.76
  (10 shorter events, 0.1 us)
Async XLA Ops:
  7.2 72.1 %copy-start = (bf16[1024,1024]{1,0:T(8,128)(2,1)S(1)}, bf16[1024,1024]{1,0:T(8,128)(2,1)}, u32[]{:S(2)}) copy-start(bf16[1024,1024]{1,0:T(8,128)(2,1)} %param.16) | copy-start | bytes 6291460
  7.2 3.8 %copy-start.4 = (bf16[4,4,4,128]{3,2,1,0:T(4,128)(2,1)S(1)}, bf16[4,4,4,128]{3,2,1,0:T(4,128)(2,1)}, u32[]{:S(2)}) copy-start(bf16[4,4,4,128]{3,2,1,0:T(4,128)(2,1)} %param.11) | copy-start | bytes 49156
  7.2 40.2 %reduce-scatter.8.cloned.1.call-start = ((), (), s32[]{:S(2)}) async-start(), calls=%async_computation.4 | async-start | bytes 163840
  9.2 17.0 %copy-start.2 = (bf16[4,4,4,128]{3,2,1,0:T(4,128)(2,1)S(1)}, bf16[4,4,4,128]{3,2,1,0:T(4,128)(2,1)}, u32[]{:S(2)}) copy-start(bf16[4,4,4,128]{3,2,1,0:T(4,128)(2,1)} %param.12) | copy-start | bytes 49156
  24.7 3.3 %copy-start.5 = (u32[32]{0:T(128)S(1)}, u32[32]{0:T(128)}, u32[]{:S(2)}) copy-start(u32[32]{0:T(128)} %constant.31) | copy-start | bytes 388
  27.3 84.2 %reduce-scatter.6.cloned.1.call-start = ((), (), s32[]{:S(2)}) async-start(), calls=%async_computation.3 | async-start | bytes 327680 | tf_op jit(solution)/shard_map/reduce_scatter | solution.py:71
  48.3 45.6 %copy-start.1 = (bf16[4,4,2048]{2,1,0:T(4,128)(2,1)S(1)}, bf16[4,4,2048]{2,1,0:T(4,128)(2,1)}, u32[]{:S(2)}) copy-start(bf16[4,4,2048]{2,1,0:T(4,128)(2,1)} %param.9) | copy-start | bytes 196612
  79.2 14.7 %copy-start.3 = (bf16[2048]{0:T(1024)(128)(2,1)S(1)}, bf16[2048]{0:T(1024)(128)(2,1)}, u32[]{:S(2)}) copy-start(bf16[2048]{0:T(1024)(128)(2,1)} %param.17) | copy-start | bytes 12292
Sparse Core Ops, SparseCore 0:
  27.4 19.9 reduce-scatter.7
  94.1 17.4 reduce-scatter.5
where the time goes:
time: 128 us; the launch traced here: 127 us
  blocking collectives  68.9 us (54%)
  waiting for transfers between devices  29.9 us (23%)
  between operations  14.9 us (12%)
  local copies, waits for them, and re-layouts  5.54 us (4%)
  matrix products  4.72 us (4%)
  other arithmetic  3.27 us (3%)
    all_gather x1, blocking collectives, on_device(): lax.all_gather(attended, 'rep', axis=0, tiled=True)  30.9 us
    reduce_scatter x1, waiting for transfers between devices, on_device(): lax.psum_scatter(partial_value.astype(jnp.bfloat16), 'tp', scatter_dimens...  17.5 us
    all_to_all x1, blocking collectives, on_device(): lax.all_to_all(projected, 'rep', split_axis=0, concat_axis=1, tiled=True)  13.5 us
    pmax x1, blocking collectives, on_device(): maxima = lax.pmax(local_maxima, 'tp')  12.9 us
    unnamed x3, waiting for transfers between devices  12.4 us
    unnamed x1, blocking collectives  5.77 us
    psum x1, blocking collectives, on_device(): squares = lax.psum(jnp.sum(hidden * hidden, axis=1), 'tp')  5.76 us
  transfers between devices with their start and end apart: 2, of which 2 were waited for; matrix products, arithmetic and copies ran while one was open for 1% of the time, Pallas kernels for 0%

commit v1 on v0

v1 whole, which is shorter than its diff:
```python
import functools
import math

import jax
import jax.numpy as jnp
from jax import lax
from jax.experimental import pallas as pl
from jax.experimental.pallas import tpu as pltpu
from jax.sharding import PartitionSpec as P

MESH = pl.DeviceIdType.MESH
PAD = 128


def kernel(
    cfg,
    lengths_ref,
    q_hbm, nk_hbm, nv_hbm, k_hbm, v_hbm, w_hbm, x_hbm, gain_hbm,
    stream_ref, normed_ref,
    q_v, k_v, v_v, w_v, x_v, gain_v,
    send_o, recv_o, send_l, recv_l,
    gathered, parts, recv_p, sq_send, sq_recv,
    load_sem, kv_sem,
    ao_send, ao_recv, al_send, al_recv, b_send, b_recv, c_send, c_recv, d_send, d_recv,
):
    n_rep, n_tp, batch, steps, heads, kv, block_len, width_all, eps = cfg
    rep = lax.axis_index("rep")
    tp = lax.axis_index("tp")
    k_own = n_rep // n_tp
    rows = batch * steps
    owned = heads // n_tp
    orow = owned * steps
    cached = block_len * kv
    fresh = steps * kv
    cw = parts.shape[2]
    hd = q_v.shape[2]
    owner = rep // k_own
    is_own = owner == tp

    loads = [pltpu.make_async_copy(q_hbm, q_v, load_sem.at[0])]
    loads[0].start()
    kv_loads = []
    for b in range(batch):
        group = [
            pltpu.make_async_copy(k_hbm.at[b], k_v.at[b, pl.ds(0, cached)], kv_sem.at[b, 0]),
            pltpu.make_async_copy(nk_hbm.at[b], k_v.at[b, pl.ds(cached, fresh)], kv_sem.at[b, 1]),
            pltpu.make_async_copy(v_hbm.at[b], v_v.at[b, pl.ds(0, cached)], kv_sem.at[b, 2]),
            pltpu.make_async_copy(nv_hbm.at[b], v_v.at[b, pl.ds(cached, fresh)], kv_sem.at[b, 3]),
        ]
        for c in group:
            c.start()
        kv_loads.append(group)
    late = [
        pltpu.make_async_copy(w_hbm, w_v, load_sem.at[1]),
        pltpu.make_async_copy(x_hbm, x_v, load_sem.at[2]),
        pltpu.make_async_copy(gain_hbm, gain_v, load_sem.at[3]),
    ]
    for c in late:
        c.start()

    barrier = pltpu.get_barrier_semaphore()
    for j in range(1, n_tp):
        pl.semaphore_signal(barrier, inc=1, device_id=(rep, lax.rem(tp + j, n_tp)), device_id_type=MESH)
    for j in range(1, n_rep):
        pl.semaphore_signal(barrier, inc=1, device_id=(lax.rem(rep + j, n_rep), tp), device_id_type=MESH)
    for i in range(k_own):
        for t in range(n_tp):
            src_rep = tp * k_own + i

            @pl.when(jnp.logical_not((src_rep == rep) & (tp == t)))
            def _():
                pl.semaphore_signal(barrier, inc=1, device_id=(src_rep, t), device_id_type=MESH)

    for b in range(batch):
        pad = jnp.zeros((PAD - fresh, hd), jnp.bfloat16)
        k_v[b, cached + fresh : cached + PAD, :] = pad
        v_v[b, cached + fresh : cached + PAD, :] = pad

    hs = heads * steps
    cols = cached + PAD
    scaling = 1.0 / math.sqrt(hd)
    row_i = lax.broadcasted_iota(jnp.int32, (hs, cols), 0)
    col_i = lax.broadcasted_iota(jnp.int32, (hs, cols), 1)
    same = (row_i // (steps * (heads // kv))) == (col_i % kv)
    is_cached = col_i < cached
    new_t = (col_i - cached) // kv
    causal = (new_t <= row_i % steps) & (col_i < cached + fresh) & (tp == 0)
    keep = same & (is_cached | causal)
    far = jnp.int32(2**30)
    position = jnp.where(keep, jnp.where(is_cached, tp * block_len + col_i // kv, -1), far)
    lane = lax.broadcasted_iota(jnp.int32, (hs, 128), 1)
    lse = jnp.zeros((hs, 128), jnp.float32)
    loads[0].wait()
    for b in range(batch):
        for c in kv_loads[b]:
            c.wait()
        s = lax.dot_general(
            q_v[b], k_v[b], (((1,), (1,)), ((), ())), preferred_element_type=jnp.float32
        )
        s = jnp.where(position < lengths_ref[b], s * scaling, -1e30)
        top = jnp.max(s, axis=1, keepdims=True)
        p = jnp.exp(s - top)
        total = jnp.sum(p, axis=1, keepdims=True)
        num = jnp.dot(p.astype(jnp.bfloat16), v_v[b], preferred_element_type=jnp.float32)
        out = (num / total).astype(jnp.bfloat16)
        for t in range(n_tp):
            send_o[t, b] = out[t * orow : (t + 1) * orow]
        lse = jnp.where(lane == b, top + jnp.log(total), lse)
    for t in range(n_tp):
        send_l[t] = lse[t * orow : (t + 1) * orow]

    arrivals = (n_tp - 1) + (n_rep - 1) + n_rep - is_own.astype(jnp.int32)
    pl.semaphore_wait(barrier, arrivals)

    sends = []
    for j in range(1, n_tp):
        peer = lax.rem(tp + j, n_tp)
        c1 = pltpu.make_async_remote_copy(
            send_l.at[peer], recv_l.at[tp], al_send.at[j], al_recv.at[tp],
            device_id=(rep, peer), device_id_type=MESH)
        c1.start()
        c2 = pltpu.make_async_remote_copy(
            send_o.at[peer], recv_o.at[tp], ao_send.at[j], ao_recv.at[tp],
            device_id=(rep, peer), device_id_type=MESH)
        c2.start()
        sends += [c1, c2]
    for j in range(1, n_tp):
        peer = lax.rem(tp + j, n_tp)
        pltpu.make_async_remote_copy(
            send_l.at[peer], recv_l.at[peer], al_send.at[j], al_recv.at[peer],
            device_id=(rep, peer), device_id_type=MESH).wait_recv()
        pltpu.make_async_remote_copy(
            send_o.at[peer], recv_o.at[peer], ao_send.at[j], ao_recv.at[peer],
            device_id=(rep, peer), device_id_type=MESH).wait_recv()
    ls = [send_l[tp]] + [recv_l[lax.rem(tp + j, n_tp)] for j in range(1, n_tp)]
    os_ = [send_o[tp]] + [recv_o[lax.rem(tp + j, n_tp)] for j in range(1, n_tp)]
    most = functools.reduce(jnp.maximum, ls)
    ws = [jnp.exp(l - most) for l in ls]
    inv = 1.0 / functools.reduce(jnp.add, ws)
    ws = [w * inv for w in ws]
    att = []
    for b in range(batch):
        acc = ws[0][:, b : b + 1] * os_[0][b].astype(jnp.float32)
        for t in range(1, n_tp):
            acc = acc + ws[t][:, b : b + 1] * os_[t][b].astype(jnp.float32)
        att.append(acc.astype(jnp.bfloat16))
    att = jnp.concatenate(att, axis=0)
    m = batch * orow
    to = lax.broadcasted_iota(jnp.int32, (m, m), 0)
    frm = lax.broadcasted_iota(jnp.int32, (m, m), 1)
    want = ((to // steps) % batch) * orow + (to // rows) * steps + to % steps
    pick = jnp.where(frm == want, 1.0, 0.0).astype(jnp.bfloat16)
    att = jnp.dot(pick, att, preferred_element_type=jnp.float32).astype(jnp.bfloat16)
    gathered[rep] = jnp.concatenate([att[h * rows : (h + 1) * rows] for h in range(owned)], axis=1)

    for j in range(1, n_rep):
        peer = lax.rem(rep + j, n_rep)
        c = pltpu.make_async_remote_copy(
            gathered.at[rep], gathered.at[rep], b_send.at[j], b_recv.at[rep],
            device_id=(peer, tp), device_id_type=MESH)
        c.start()
        sends.append(c)
    late[0].wait()
    for j in range(1, n_rep):
        peer = lax.rem(rep + j, n_rep)
        pltpu.make_async_remote_copy(
            gathered.at[peer], gathered.at[peer], b_send.at[j], b_recv.at[peer],
            device_id=(peer, tp), device_id_type=MESH).wait_recv()
    full = gathered[...].reshape(n_rep * rows, gathered.shape[2])
    proj = jnp.dot(full, w_v[...], preferred_element_type=jnp.float32).astype(jnp.bfloat16)
    parts[...] = proj.reshape(n_rep, rows, cw)

    slot = lax.rem(rep, k_own) * n_tp + tp
    for j in range(1, n_rep):
        peer = lax.rem(rep + j, n_rep)
        c = pltpu.make_async_remote_copy(
            parts.at[peer], recv_p.at[slot], c_send.at[j], c_recv.at[slot],
            device_id=(peer, owner), device_id_type=MESH)
        c.start()
        sends.append(c)
    mine = pltpu.make_async_remote_copy(
        parts.at[rep], recv_p.at[slot], c_send.at[0], c_recv.at[slot],
        device_id=(rep, owner), device_id_type=MESH)

    @pl.when(is_own)
    def _():
        recv_p[slot] = parts[rep]

    @pl.when(jnp.logical_not(is_own))
    def _():
        mine.start()

    late[1].wait()
    late[2].wait()
    for i in range(k_own):
        for t in range(n_tp):
            sid = i * n_tp + t
            src_rep = tp * k_own + i

            @pl.when(jnp.logical_not((src_rep == rep) & (tp == t)))
            def _():
                pltpu.make_async_remote_copy(
                    parts.at[0], recv_p.at[sid], c_send.at[0], c_recv.at[sid],
                    device_id=(src_rep, t), device_id_type=MESH).wait_recv()

    pieces = []
    for i in range(k_own):
        acc = recv_p[i * n_tp].astype(jnp.float32)
        for t in range(1, n_tp):
            acc = acc + recv_p[i * n_tp + t].astype(jnp.float32)
        pieces.append(acc)
    summed = jnp.concatenate(pieces, axis=1)
    x = x_v[...].astype(jnp.float32).reshape(rows, x_v.shape[2])
    hidden = x + summed
    squares = jnp.sum(hidden * hidden, axis=1, keepdims=True)

    sq_send[...] = jnp.broadcast_to(squares, sq_send.shape)
    for j in range(1, n_tp):
        peer = lax.rem(tp + j, n_tp)
        c = pltpu.make_async_remote_copy(
            sq_send, sq_recv.at[tp], d_send.at[j], d_recv.at[tp],
            device_id=(rep, peer), device_id_type=MESH)
        c.start()
        sends.append(c)
    stream_ref[...] = hidden.astype(jnp.bfloat16).reshape(stream_ref.shape)
    gained = hidden * gain_v[...].astype(jnp.float32)
    every = sq_send[...]
    for j in range(1, n_tp):
        peer = lax.rem(tp + j, n_tp)
        pltpu.make_async_remote_copy(
            sq_send, sq_recv.at[peer], d_send.at[j], d_recv.at[peer],
            device_id=(rep, peer), device_id_type=MESH).wait_recv()
        every = every + sq_recv[peer]
    inverse = lax.rsqrt(every[:, :1] / width_all + eps)
    normed_ref[...] = (gained * inverse).astype(jnp.bfloat16).reshape(normed_ref.shape)

    for c in sends:
        c.wait_send()

    @pl.when(jnp.logical_not(is_own))
    def _():
        mine.wait_send()


def on_device(
    n_rep, n_tp,
    stream_in, queries, new_keys, new_values, key_cache, value_cache, lengths, out_weight, norm_gain
):
    batch, steps, width = queries.shape
    block_len, kv, hd = key_cache.shape[1:]
    heads = width // hd
    depth, cw = out_weight.shape
    own_w = stream_in.shape[2]
    rows = batch * steps
    assert n_rep % n_tp == 0 and heads % n_tp == 0
    owned = heads // n_tp
    orow = owned * steps
    hs = heads * steps
    cached = block_len * kv
    q = queries.reshape(batch, steps, heads, hd).transpose(0, 2, 1, 3).reshape(batch, hs, hd)
    nk = new_keys.reshape(batch, steps * kv, hd)
    nv = new_values.reshape(batch, steps * kv, hd)
    kc = key_cache.reshape(batch, cached, hd)
    vc = value_cache.reshape(batch, cached, hd)
    cfg = (n_rep, n_tp, batch, steps, heads, kv, block_len, own_w * n_tp, 1e-6)
    bf, f32 = jnp.bfloat16, jnp.float32
    anyspec = pl.BlockSpec(memory_space=pl.ANY)
    dma = pltpu.SemaphoreType.DMA
    return pl.pallas_call(
        functools.partial(kernel, cfg),
        out_shape=(
            jax.ShapeDtypeStruct(stream_in.shape, bf),
            jax.ShapeDtypeStruct(stream_in.shape, bf),
        ),
        in_specs=[pl.BlockSpec(memory_space=pltpu.SMEM)] + [anyspec] * 8,
        out_specs=(pl.BlockSpec(memory_space=pltpu.VMEM), pl.BlockSpec(memory_space=pltpu.VMEM)),
        scratch_shapes=[
            pltpu.VMEM((batch, hs, hd), bf),
            pltpu.VMEM((batch, cached + PAD, hd), bf),
            pltpu.VMEM((batch, cached + PAD, hd), bf),
            pltpu.VMEM((depth, cw), bf),
            pltpu.VMEM((batch, steps, own_w), bf),
            pltpu.VMEM((1, own_w), bf),
            pltpu.VMEM((n_tp, batch, orow, hd), bf),
            pltpu.VMEM((n_tp, batch, orow, hd), bf),
            pltpu.VMEM((n_tp, orow, 128), f32),
            pltpu.VMEM((n_tp, orow, 128), f32),
            pltpu.VMEM((n_rep, rows, depth), bf),
            pltpu.VMEM((n_rep, rows, cw), bf),
            pltpu.VMEM((n_rep, rows, cw), bf),
            pltpu.VMEM((rows, 128), f32),
            pltpu.VMEM((n_tp, rows, 128), f32),
            dma((4,)),
            dma((batch, 4)),
            dma((n_tp,)), dma((n_tp,)), dma((n_tp,)), dma((n_tp,)),
            dma((n_rep,)), dma((n_rep,)), dma((n_rep,)), dma((n_rep,)),
            dma((n_tp,)), dma((n_tp,)),
        ],
        compiler_params=pltpu.CompilerParams(collective_id=0, has_side_effects=True),
    )(lengths, q, nk, nv, kc, vc, out_weight, stream_in, norm_gain.reshape(1, own_w))


def solution(mesh):
    return jax.shard_map(
        functools.partial(on_device, mesh.shape["rep"], mesh.shape["tp"]),
        mesh=mesh,
        in_specs=(
            P("rep", None, "tp"),
            P("rep", None, None),
            P("rep", None, None, None),
            P("rep", None, None, None),
            P("rep", "tp", None, None),
            P("rep", "tp", None, None),
            P("rep"),
            P("tp", "rep"),
            P("tp"),
        ),
        out_specs=(P("rep", None, "tp"), P("rep", None, "tp")),
        check_vma=False,
    )
```

time: 128 us -> 35.6 us (0.28)
  blocking collectives: 68.9 us -> 0 us
  Pallas kernels: 0 us -> 30.4 us
  waiting for transfers between devices: 29.9 us -> 0 us
  between operations: 14.9 us -> 0.64 us
  matrix products: 4.72 us -> 0 us
  other arithmetic: 3.27 us -> 0 us
    all_gather x1 -> x0, blocking collectives: 30.9 us -> none  [on_device(): lax.all_gather(attended, 'rep', axis=0, tiled=True)]
    pallas_call x0 -> x1, Pallas kernels: none -> 30.4 us  [on_device(): pl.pallas_call(functools.partial(kernel, cfg), out_shape=(jax.ShapeDtypeS...]
    reduce_scatter x1 -> x0, waiting for transfers between devices: 17.5 us -> none  [on_device(): lax.psum_scatter(partial_value.astype(jnp.bfloat16), 'tp', scatter_dimens...]
    all_to_all x1 -> x0, blocking collectives: 13.5 us -> none  [on_device(): lax.all_to_all(projected, 'rep', split_axis=0, concat_axis=1, tiled=True)]
    pmax x1 -> x0, blocking collectives: 12.9 us -> none  [on_device(): maxima = lax.pmax(local_maxima, 'tp')]
    unnamed x3 -> x0, waiting for transfers between devices: 12.4 us -> none
    unnamed x1 -> x0, blocking collectives: 5.77 us -> none
    psum x1 -> x0, blocking collectives: 5.76 us -> none  [on_device(): squares = lax.psum(jnp.sum(hidden * hidden, axis=1), 'tp')]
  transfers between devices with their start and end apart: 2 -> 0, of which waited for: 2 -> 0; matrix products, arithmetic and copies ran while one was open for 1% -> 0% of each run, Pallas kernels for 0% -> 0%
where the time goes in v1:
time: 35.6 us; the launch traced here: 35.3 us
  Pallas kernels  30.4 us (85%)
  local copies, waits for them, and re-layouts  4.28 us (12%)
  between operations  0.64 us (2%)
    pallas_call x1, Pallas kernels, on_device(): pl.pallas_call(functools.partial(kernel, cfg), out_shape=(jax.ShapeDtypeS...  30.4 us
    unnamed x2, local copies, waits for them, and re-layouts  2.98 us
    reshape x1, local copies, waits for them, and re-layouts, on_device(): norm_gain.reshape(1, own_w)  1.29 us

profile of v1, /device:TPU:0, one launch (start us, length us, event | category | flops | bytes accessed | tf_op | source)
XLA Modules:
  0.0 35.3 jit_solution(16608878466761007943)
XLA Ops:
  0.6 1.3 %reshape.31.gain_hbm = bf16[1,2048]{1,0:T(2,128)(2,1)} reshape(bf16[2048]{0:T(1024)(128)(2,1)} %param.17) | data formatting | bytes 8192 | tf_op jit(solution)/shard_map/reshape | solution.py:300
  1.9 30.4 %shard_map.104 = (bf16[4,4,2048]{2,1,0:T(4,128)(2,1)}, bf16[4,4,2048]{2,1,0:T(4,128)(2,1)}) custom-call(s32[4]{0:T(128)} %lengths_ref.1, bf16[4,128,128]{2,1,0:T(8,128)(2,1)} %bitcast.11, bf16[4,16,128]{2,1,0:T(8,128)(2,1)} %bitcast.12, bf16[4,16,128]{2,1,0:T(8,128)(2,1)} %bitcast.13, bf16[4,1024,128]{2,1,0:T(8,128)(2,1)} %bitcast.9, ...), custom_call_target="tpu_custom_call" | custom-call | tf_op jit(solution)/shard_map/pallas_call | solution.py:269
  32.4 1.5 %copy.14 = bf16[4,4,2048]{2,1,0:T(4,128)(2,1)} copy(bf16[4,4,2048]{2,1,0:T(4,128)(2,1)} %get-tuple-element.4) | data formatting | bytes 131072
  33.9 1.5 %copy.15 = bf16[4,4,2048]{2,1,0:T(4,128)(2,1)} copy(bf16[4,4,2048]{2,1,0:T(4,128)(2,1)} %get-tuple-element.5) | data formatting | bytes 131072

commit v2 on v1

--- a/solution.py
+++ b/solution.py
@@ -10,6 +10,16 @@
 
 MESH = pl.DeviceIdType.MESH
 PAD = 128
+
+
+def flip(index, mask, count):
+    other = 0
+    bit = 1
+    while bit < count:
+        digit = (index // bit) % 2
+        other = other + bit * ((1 - digit) if mask & bit else digit)
+        bit *= 2
+    return other
 
 
 def kernel(
@@ -37,6 +47,22 @@
     owner = rep // k_own
     is_own = owner == tp
 
+    sends = []
+    half = batch // 2 if batch % 2 == 0 else batch
+    parts_a = batch // half
+    barrier = pltpu.get_barrier_semaphore()
+    for j in range(1, n_tp):
+        pl.semaphore_signal(barrier, inc=1, device_id=(rep, lax.rem(tp + j, n_tp)), device_id_type=MESH)
+    for j in range(1, n_rep):
+        pl.semaphore_signal(barrier, inc=1, device_id=(lax.rem(rep + j, n_rep), tp), device_id_type=MESH)
+    for i in range(k_own):
+        for t in range(n_tp):
+            src_rep = tp * k_own + i
+
+            @pl.when(jnp.logical_not((src_rep == rep) & (tp == t)))
+            def _():
+                pl.semaphore_signal(barrier, inc=1, device_id=(src_rep, t), device_id_type=MESH)
+
     loads = [pltpu.make_async_copy(q_hbm, q_v, load_sem.at[0])]
     loads[0].start()
     kv_loads = []
@@ -57,19 +83,6 @@
     ]
     for c in late:
         c.start()
-
-    barrier = pltpu.get_barrier_semaphore()
-    for j in range(1, n_tp):
-        pl.semaphore_signal(barrier, inc=1, device_id=(rep, lax.rem(tp + j, n_tp)), device_id_type=MESH)
-    for j in range(1, n_rep):
-        pl.semaphore_signal(barrier, inc=1, device_id=(lax.rem(rep + j, n_rep), tp), device_id_type=MESH)
-    for i in range(k_own):
-        for t in range(n_tp):
-            src_rep = tp * k_own + i
-
-            @pl.when(jnp.logical_not((src_rep == rep) & (tp == t)))
-            def _():
-                pl.semaphore_signal(barrier, inc=1, device_id=(src_rep, t), device_id_type=MESH)
 
     for b in range(batch):
         pad = jnp.zeros((PAD - fresh, hd), jnp.bfloat16)
@@ -106,32 +119,39 @@
         for t in range(n_tp):
             send_o[t, b] = out[t * orow : (t + 1) * orow]
         lse = jnp.where(lane == b, top + jnp.log(total), lse)
-    for t in range(n_tp):
-        send_l[t] = lse[t * orow : (t + 1) * orow]
-
-    arrivals = (n_tp - 1) + (n_rep - 1) + n_rep - is_own.astype(jnp.int32)
-    pl.semaphore_wait(barrier, arrivals)
-
-    sends = []
-    for j in range(1, n_tp):
-        peer = lax.rem(tp + j, n_tp)
-        c1 = pltpu.make_async_remote_copy(
-            send_l.at[peer], recv_l.at[tp], al_send.at[j], al_recv.at[tp],
-            device_id=(rep, peer), device_id_type=MESH)
-        c1.start()
-        c2 = pltpu.make_async_remote_copy(
-            send_o.at[peer], recv_o.at[tp], ao_send.at[j], ao_recv.at[tp],
-            device_id=(rep, peer), device_id_type=MESH)
-        c2.start()
-        sends += [c1, c2]
+        if (b + 1) % half == 0:
+            part = b // half
+            if part == 0:
+                arrivals = (n_tp - 1) + (n_rep - 1) + n_rep - is_own.astype(jnp.int32)
+                pl.semaphore_wait(barrier, arrivals)
+            if part == parts_a - 1:
+                for t in range(n_tp):
+                    send_l[t] = lse[t * orow : (t + 1) * orow]
+            span = pl.ds(part * half, half)
+            for j in range(1, n_tp):
+                peer = lax.rem(tp + j, n_tp)
+                if part == parts_a - 1:
+                    c = pltpu.make_async_remote_copy(
+                        send_l.at[peer], recv_l.at[tp], al_send.at[j], al_recv.at[tp],
+                        device_id=(rep, peer), device_id_type=MESH)
+                    c.start()
+                    sends.append(c)
+                c = pltpu.make_async_remote_copy(
+                    send_o.at[peer, span], recv_o.at[tp, span], ao_send.at[part, j], ao_recv.at[part, tp],
+                    device_id=(rep, peer), device_id_type=MESH)
+                c.start()
+                sends.append(c)
+
     for j in range(1, n_tp):
         peer = lax.rem(tp + j, n_tp)
         pltpu.make_async_remote_copy(
             send_l.at[peer], recv_l.at[peer], al_send.at[j], al_recv.at[peer],
             device_id=(rep, peer), device_id_type=MESH).wait_recv()
-        pltpu.make_async_remote_copy(
-            send_o.at[peer], recv_o.at[peer], ao_send.at[j], ao_recv.at[peer],
-            device_id=(rep, peer), device_id_type=MESH).wait_recv()
+        for part in range(parts_a):
+            span = pl.ds(part * half, half)
+            pltpu.make_async_remote_copy(
+                send_o.at[peer, span], recv_o.at[peer, span], ao_send.at[part, j], ao_recv.at[part, peer],
+                device_id=(rep, peer), device_id_type=MESH).wait_recv()
     ls = [send_l[tp]] + [recv_l[lax.rem(tp + j, n_tp)] for j in range(1, n_tp)]
     os_ = [send_o[tp]] + [recv_o[lax.rem(tp + j, n_tp)] for j in range(1, n_tp)]
     most = functools.reduce(jnp.maximum, ls)
@@ -153,34 +173,36 @@
     att = jnp.dot(pick, att, preferred_element_type=jnp.float32).astype(jnp.bfloat16)
     gathered[rep] = jnp.concatenate([att[h * rows : (h + 1) * rows] for h in range(owned)], axis=1)
 
-    for j in range(1, n_rep):
-        peer = lax.rem(rep + j, n_rep)
+    for mask in range(n_rep - 1, 0, -1):
+        peer = flip(rep, mask, n_rep)
         c = pltpu.make_async_remote_copy(
-            gathered.at[rep], gathered.at[rep], b_send.at[j], b_recv.at[rep],
+            gathered.at[rep], gathered.at[rep], b_send.at[mask], b_recv.at[rep],
             device_id=(peer, tp), device_id_type=MESH)
         c.start()
         sends.append(c)
     late[0].wait()
-    for j in range(1, n_rep):
-        peer = lax.rem(rep + j, n_rep)
-        pltpu.make_async_remote_copy(
-            gathered.at[peer], gathered.at[peer], b_send.at[j], b_recv.at[peer],
-            device_id=(peer, tp), device_id_type=MESH).wait_recv()
-    full = gathered[...].reshape(n_rep * rows, gathered.shape[2])
-    proj = jnp.dot(full, w_v[...], preferred_element_type=jnp.float32).astype(jnp.bfloat16)
-    parts[...] = proj.reshape(n_rep, rows, cw)
-
     slot = lax.rem(rep, k_own) * n_tp + tp
-    for j in range(1, n_rep):
-        peer = lax.rem(rep + j, n_rep)
-        c = pltpu.make_async_remote_copy(
-            parts.at[peer], recv_p.at[slot], c_send.at[j], c_recv.at[slot],
-            device_id=(peer, owner), device_id_type=MESH)
-        c.start()
-        sends.append(c)
     mine = pltpu.make_async_remote_copy(
         parts.at[rep], recv_p.at[slot], c_send.at[0], c_recv.at[slot],
         device_id=(rep, owner), device_id_type=MESH)
+    for pair in range(n_rep // 2 - 1, -1, -1):
+        masks = (2 * pair + 1, 2 * pair)
+        peers = [flip(rep, mask, n_rep) for mask in masks]
+        for mask, peer in zip(masks, peers):
+            if mask:
+                pltpu.make_async_remote_copy(
+                    gathered.at[peer], gathered.at[peer], b_send.at[mask], b_recv.at[peer],
+                    device_id=(peer, tp), device_id_type=MESH).wait_recv()
+        block = jnp.concatenate([gathered[peer] for peer in peers], axis=0)
+        proj = jnp.dot(block, w_v[...], preferred_element_type=jnp.float32).astype(jnp.bfloat16)
+        for i, (mask, peer) in enumerate(zip(masks, peers)):
+            parts[peer] = proj[i * rows : (i + 1) * rows]
+            if mask:
+                c = pltpu.make_async_remote_copy(
+                    parts.at[peer], recv_p.at[slot], c_send.at[mask], c_recv.at[slot],
+                    device_id=(peer, owner), device_id_type=MESH)
+                c.start()
+                sends.append(c)
 
     @pl.when(is_own)
     def _():
@@ -192,6 +214,9 @@
 
     late[1].wait()
     late[2].wait()
+    gain = gain_v[...].astype(jnp.float32)
+    gain = jnp.concatenate([gain[c : c + 1] for c in range(gain.shape[0])], axis=1)
+    x = x_v[...].astype(jnp.float32).reshape(rows, x_v.shape[2])
     for i in range(k_own):
         for t in range(n_tp):
             sid = i * n_tp + t
@@ -210,7 +235,6 @@
             acc = acc + recv_p[i * n_tp + t].astype(jnp.float32)
         pieces.append(acc)
     summed = jnp.concatenate(pieces, axis=1)
-    x = x_v[...].astype(jnp.float32).reshape(rows, x_v.shape[2])
     hidden = x + summed
     squares = jnp.sum(hidden * hidden, axis=1, keepdims=True)
 
@@ -223,7 +247,7 @@
         c.start()
         sends.append(c)
     stream_ref[...] = hidden.astype(jnp.bfloat16).reshape(stream_ref.shape)
-    gained = hidden * gain_v[...].astype(jnp.float32)
+    gained = hidden * gain
     every = sq_send[...]
     for j in range(1, n_tp):
         peer = lax.rem(tp + j, n_tp)
@@ -252,6 +276,7 @@
     depth, cw = out_weight.shape
     own_w = stream_in.shape[2]
     rows = batch * steps
+    assert n_rep & (n_rep - 1) == 0
     assert n_rep % n_tp == 0 and heads % n_tp == 0
     owned = heads // n_tp
     orow = owned * steps
@@ -269,8 +294,8 @@
     return pl.pallas_call(
         functools.partial(kernel, cfg),
         out_shape=(
-            jax.ShapeDtypeStruct(stream_in.shape, bf),
-            jax.ShapeDtypeStruct(stream_in.shape, bf),
+            pltpu.VMEM(stream_in.shape, bf),
+            pltpu.VMEM(stream_in.shape, bf),
         ),
         in_specs=[pl.BlockSpec(memory_space=pltpu.SMEM)] + [anyspec] * 8,
         out_specs=(pl.BlockSpec(memory_space=pltpu.VMEM), pl.BlockSpec(memory_space=pltpu.VMEM)),
@@ -280,7 +305,7 @@
             pltpu.VMEM((batch, cached + PAD, hd), bf),
             pltpu.VMEM((depth, cw), bf),
             pltpu.VMEM((batch, steps, own_w), bf),
-            pltpu.VMEM((1, own_w), bf),
+            pltpu.VMEM((own_w // 128, 128), bf),
             pltpu.VMEM((n_tp, batch, orow, hd), bf),
             pltpu.VMEM((n_tp, batch, orow, hd), bf),
             pltpu.VMEM((n_tp, orow, 128), f32),
@@ -292,12 +317,12 @@
             pltpu.VMEM((n_tp, rows, 128), f32),
             dma((4,)),
             dma((batch, 4)),
-            dma((n_tp,)), dma((n_tp,)), dma((n_tp,)), dma((n_tp,)),
+            dma((batch, n_tp)), dma((batch, n_tp)), dma((n_tp,)), dma((n_tp,)),
             dma((n_rep,)), dma((n_rep,)), dma((n_rep,)), dma((n_rep,)),
             dma((n_tp,)), dma((n_tp,)),
         ],
         compiler_params=pltpu.CompilerParams(collective_id=0, has_side_effects=True),
-    )(lengths, q, nk, nv, kc, vc, out_weight, stream_in, norm_gain.reshape(1, own_w))
+    )(lengths, q, nk, nv, kc, vc, out_weight, stream_in, norm_gain.reshape(own_w // 128, 128))
 
 
 def solution(mesh):

time: 35.6 us -> 31.1 us (0.87)
  local copies, waits for them, and re-layouts: 4.28 us -> 1.26 us
  Pallas kernels: 30.4 us -> 29.1 us
    unnamed x2, local copies, waits for them, and re-layouts: 2.98 us -> 1.26 us
    pallas_call x1, Pallas kernels: 30.4 us -> 29.1 us  [on_device(): pl.pallas_call(functools.partial(kernel, cfg), out_shape=(pltpu.VMEM(stre...]
    reshape x1 -> x0, local copies, waits for them, and re-layouts: 1.29 us -> none  [on_device(): norm_gain.reshape(1, own_w)]
where the time goes in v2:
time: 31.1 us; the launch traced here: 31 us
  Pallas kernels  29.1 us (94%)
  local copies, waits for them, and re-layouts  1.26 us (4%)
  between operations  0.64 us (2%)
    pallas_call x1, Pallas kernels, on_device(): pl.pallas_call(functools.partial(kernel, cfg), out_shape=(pltpu.VMEM(stre...  29.1 us
    unnamed x2, local copies, waits for them, and re-layouts  1.26 us

profile of v2, /device:TPU:0, one launch (start us, length us, event | category | flops | bytes accessed | tf_op | source)
XLA Modules:
  0.0 31.0 jit_solution(11691204857285958877)
XLA Ops:
  0.6 29.1 %shard_map.104 = (bf16[4,4,2048]{2,1,0:T(4,128)(2,1)S(1)}, bf16[4,4,2048]{2,1,0:T(4,128)(2,1)S(1)}) custom-call(s32[4]{0:T(128)} %lengths_ref.1, bf16[4,128,128]{2,1,0:T(8,128)(2,1)} %bitcast.12, bf16[4,16,128]{2,1,0:T(8,128)(2,1)} %bitcast.13, bf16[4,16,128]{2,1,0:T(8,128)(2,1)} %bitcast.14, bf16[4,1024,128]{2,1,0:T(8,128)(2,1)} %bitcast.10, ...), custom_call_target="tpu_custom_call" | custom-call | tf_op jit(solution)/shard_map/pallas_call | solution.py:294
  29.7 0.6 %copy.14 = bf16[4,4,2048]{2,1,0:T(4,128)(2,1)} copy(bf16[4,4,2048]{2,1,0:T(4,128)(2,1)S(1)} %get-tuple-element.2) | data formatting | bytes 131072
  30.3 0.6 %copy.15 = bf16[4,4,2048]{2,1,0:T(4,128)(2,1)} copy(bf16[4,4,2048]{2,1,0:T(4,128)(2,1)S(1)} %get-tuple-element.3) | data formatting | bytes 131072

commit v3 on v2

--- a/solution.py
+++ b/solution.py
@@ -26,7 +26,7 @@
     cfg,
     lengths_ref,
     q_hbm, nk_hbm, nv_hbm, k_hbm, v_hbm, w_hbm, x_hbm, gain_hbm,
-    stream_ref, normed_ref,
+    hidden_ref, scale_ref,
     q_v, k_v, v_v, w_v, x_v, gain_v,
     send_o, recv_o, send_l, recv_l,
     gathered, parts, recv_p, sq_send, sq_recv,
@@ -173,7 +173,10 @@
     att = jnp.dot(pick, att, preferred_element_type=jnp.float32).astype(jnp.bfloat16)
     gathered[rep] = jnp.concatenate([att[h * rows : (h + 1) * rows] for h in range(owned)], axis=1)
 
-    for mask in range(n_rep - 1, 0, -1):
+    pairs = n_rep // 2
+    mid = pairs // 2
+    order = [mid, *range(mid - 1, 0, -1), *range(pairs - 1, mid, -1), 0] if mid else [0]
+    for mask in [m for pair in order for m in (2 * pair + 1, 2 * pair) if m]:
         peer = flip(rep, mask, n_rep)
         c = pltpu.make_async_remote_copy(
             gathered.at[rep], gathered.at[rep], b_send.at[mask], b_recv.at[rep],
@@ -185,7 +188,7 @@
     mine = pltpu.make_async_remote_copy(
         parts.at[rep], recv_p.at[slot], c_send.at[0], c_recv.at[slot],
         device_id=(rep, owner), device_id_type=MESH)
-    for pair in range(n_rep // 2 - 1, -1, -1):
+    for pair in order:
         masks = (2 * pair + 1, 2 * pair)
         peers = [flip(rep, mask, n_rep) for mask in masks]
         for mask, peer in zip(masks, peers):
@@ -246,8 +249,7 @@
             device_id=(rep, peer), device_id_type=MESH)
         c.start()
         sends.append(c)
-    stream_ref[...] = hidden.astype(jnp.bfloat16).reshape(stream_ref.shape)
-    gained = hidden * gain
+    hidden_ref[...] = hidden.reshape(hidden_ref.shape)
     every = sq_send[...]
     for j in range(1, n_tp):
         peer = lax.rem(tp + j, n_tp)
@@ -256,7 +258,7 @@
             device_id=(rep, peer), device_id_type=MESH).wait_recv()
         every = every + sq_recv[peer]
     inverse = lax.rsqrt(every[:, :1] / width_all + eps)
-    normed_ref[...] = (gained * inverse).astype(jnp.bfloat16).reshape(normed_ref.shape)
+    scale_ref[...] = (inverse * gain).reshape(scale_ref.shape)
 
     for c in sends:
         c.wait_send()
@@ -291,11 +293,11 @@
     bf, f32 = jnp.bfloat16, jnp.float32
     anyspec = pl.BlockSpec(memory_space=pl.ANY)
     dma = pltpu.SemaphoreType.DMA
-    return pl.pallas_call(
+    hidden, scale = pl.pallas_call(
         functools.partial(kernel, cfg),
         out_shape=(
-            pltpu.VMEM(stream_in.shape, bf),
-            pltpu.VMEM(stream_in.shape, bf),
+            pltpu.VMEM(stream_in.shape, f32),
+            pltpu.VMEM(stream_in.shape, f32),
         ),
         in_specs=[pl.BlockSpec(memory_space=pltpu.SMEM)] + [anyspec] * 8,
         out_specs=(pl.BlockSpec(memory_space=pltpu.VMEM), pl.BlockSpec(memory_space=pltpu.VMEM)),
@@ -323,6 +325,7 @@
         ],
         compiler_params=pltpu.CompilerParams(collective_id=0, has_side_effects=True),
     )(lengths, q, nk, nv, kc, vc, out_weight, stream_in, norm_gain.reshape(own_w // 128, 128))
+    return (hidden.astype(bf), (hidden * scale).astype(bf))
 
 
 def solution(mesh):

time: 31.1 us -> 29.5 us (0.949)
  local copies, waits for them, and re-layouts: 1.26 us -> 0 us
  Pallas kernels: 29.1 us -> 28 us
  other arithmetic: 0 us -> 0.7 us
    unnamed x2 -> x0, local copies, waits for them, and re-layouts: 1.26 us -> none
    pallas_call x1, Pallas kernels: 29.1 us -> 28 us  [on_device(): pl.pallas_call(functools.partial(kernel, cfg), out_shape=(pltpu.VMEM(stre...]
    convert_element_type x0 -> x1, other arithmetic: none -> 0.7 us  [on_device(): return (hidden.astype(bf), (hidden * scale).astype(bf))]
where the time goes in v3:
time: 29.5 us; the launch traced here: 29.3 us
  Pallas kernels  28 us (95%)
  other arithmetic  0.7 us (2%)
  between operations  0.64 us (2%)
    pallas_call x1, Pallas kernels, on_device(): pl.pallas_call(functools.partial(kernel, cfg), out_shape=(pltpu.VMEM(stre...  28 us
    convert_element_type x1, other arithmetic, on_device(): return (hidden.astype(bf), (hidden * scale).astype(bf))  0.7 us

profile of v3, /device:TPU:0, one launch (start us, length us, event | category | flops | bytes accessed | tf_op | source)
XLA Modules:
  0.0 29.3 jit_solution(9607801668822992945)
XLA Ops:
  0.6 28.0 %shard_map.104 = (f32[4,4,2048]{2,1,0:T(4,128)S(1)}, f32[4,4,2048]{2,1,0:T(4,128)S(1)}) custom-call(s32[4]{0:T(128)} %lengths_ref.1, bf16[4,128,128]{2,1,0:T(8,128)(2,1)} %bitcast.12, bf16[4,16,128]{2,1,0:T(8,128)(2,1)} %bitcast.13, bf16[4,16,128]{2,1,0:T(8,128)(2,1)} %bitcast.14, bf16[4,1024,128]{2,1,0:T(8,128)(2,1)} %bitcast.10, ...), custom_call_target="tpu_custom_call" | custom-call | tf_op jit(solution)/shard_map/pallas_call | solution.py:296
  28.6 0.7 %multiply_convert_fusion = (bf16[4,4,2048]{2,1,0:T(4,128)(2,1)}, bf16[4,4,2048]{2,1,0:T(4,128)(2,1)}) fusion(f32[4,4,2048]{2,1,0:T(4,128)S(1)} %get-tuple-element.4, f32[4,4,2048]{2,1,0:T(4,128)S(1)} %get-tuple-element.5), kind=kLoop, calls=%fused_computation | loop fusion | flops 98304 | bytes 393216 | tf_op jit(solution)/shard_map/convert_element_type | solution.py:328
